TPU v7x, 256 devices: a whole 4x4x8 slice. The times are simulated.
256 devices in a mesh: group: 4 (over x), dp: 16 (over z_lo, y, core), mp: 4 (over z_hi).
Axes of the slice: x: 4, y: 4, z: 8 (z_hi: 4, z_lo: 2; z = z_hi * 2 + z_lo), core: 2. Of those that a mesh axis runs over, the one named last changes fastest.
Arguments:
- block_input: bfloat16 [768, 8192], P(None, 'dp'), may hold values from -6 to 6
- parent_gate_up: bfloat16 [2, 8192, 14336], P(None, 'dp', ('group', 'mp')), may hold values from -0.0625 to 0.0625
- parent_down: bfloat16 [14336, 8192], P(('group', 'mp'), 'dp'), may hold values from -0.046875 to 0.046875
- variant_gate_up: bfloat16 [4, 2, 8192, 3584], P('group', None, 'dp', 'mp'), may hold values from -0.0625 to 0.0625
- variant_down: bfloat16 [4, 3584, 8192], P('group', 'mp', 'dp'), may hold values from -0.09375 to 0.09375
- widths: int32 [4], P('group'), may hold values from 896 to 3584, as said below
Outputs:
- grad_gate_up: float32 [4, 2, 8192, 3584], P('group', None, 'dp', 'mp')
- grad_down: float32 [4, 3584, 8192], P('group', 'mp', 'dp')
Inputs may be any that keep to these rules, and one draw needn't show every extreme that they name: Variant v uses its hidden units 0 to widths[v] - 1; one variant uses all 3584 of them and another exactly a quarter of 3584.
All inputs are finite; a program needn't handle non-finite values.
Results may differ from a plain program's by a relative error of at most 0.008.
Values may be sent and summed in bfloat16 or wider, within the bound.
No kernel may reach another device: no remote copies, remote signals or barrier semaphores. Data moves between devices by JAX's collectives and lax.ppermute only.
A program may use at most 64 MiB of HBM per device.

v0:
```python
import math
import jax
import jax.numpy as jnp
from jax import lax
from jax.sharding import PartitionSpec as P


def gated_values(pre_act, unit_mask):
    gate_value = pre_act[:, 0].astype(jnp.float32)
    up_value = pre_act[:, 1].astype(jnp.float32)
    sigmoid_gate = jax.nn.sigmoid(gate_value)
    return (gate_value * sigmoid_gate * up_value * unit_mask).astype(jnp.bfloat16)


def pre_gradient(pre_act, unit_mask, hidden_grad):
    gate_value = pre_act[:, 0].astype(jnp.float32)
    up_value = pre_act[:, 1].astype(jnp.float32)
    sigmoid_gate = jax.nn.sigmoid(gate_value)
    masked_grad = hidden_grad * unit_mask
    grad_gate = masked_grad * up_value * sigmoid_gate * (1.0 + gate_value * (1.0 - sigmoid_gate))
    grad_up = masked_grad * gate_value * sigmoid_gate
    return jnp.stack([grad_gate, grad_up], axis=1).astype(jnp.bfloat16)


def body(block_input, parent_gate_up, parent_down, variant_gate_up, variant_down, widths):
    local_gate_up = variant_gate_up[0]
    local_down = variant_down[0]
    local_units = local_down.shape[0]
    all_tokens = block_input.shape[0]
    first_unit = lax.axis_index("mp") * local_units
    unit_index = first_unit + jnp.arange(local_units, dtype=jnp.int32)
    unit_mask = (unit_index < widths[0]).astype(jnp.float32)
    parent_term = jnp.einsum(
        "td,kdf->tkf", block_input, parent_gate_up, preferred_element_type=jnp.float32
    )
    variant_term = jnp.einsum(
        "td,kdf->tkf", block_input, local_gate_up, preferred_element_type=jnp.float32
    )
    parent_rows, variant_rows = (
        lax.psum_scatter(parent_term, "dp", scatter_dimension=0, tiled=True),
        lax.psum_scatter(variant_term, "dp", scatter_dimension=0, tiled=True),
    )
    parent_pre = parent_rows.astype(jnp.bfloat16)
    variant_pre = variant_rows.astype(jnp.bfloat16)
    parent_hidden = gated_values(parent_pre, 1.0)
    parent_all, variant_all = (
        lax.all_gather(parent_hidden, "dp", axis=0, tiled=True),
        lax.all_gather(variant_pre, "dp", axis=0, tiled=True),
    )
    variant_hidden = gated_values(variant_all, unit_mask)
    teacher_part = jnp.dot(parent_all, parent_down, preferred_element_type=jnp.float32)
    student_part = jnp.dot(variant_hidden, local_down, preferred_element_type=jnp.float32)
    teacher = lax.psum(teacher_part, ("group", "mp"))
    student = lax.psum(student_part, "mp")
    loss_scale = 1.0 / math.sqrt(all_tokens)
    output_grad = ((student - teacher) * loss_scale).astype(jnp.bfloat16)
    grad_down = lax.dot_general(
        variant_hidden, output_grad, (((0,), (0,)), ((), ())), preferred_element_type=jnp.float32
    )
    hidden_part = lax.dot_general(
        output_grad, local_down, (((1,), (1,)), ((), ())), preferred_element_type=jnp.float32
    )
    hidden_full = lax.psum(hidden_part, "dp")
    grad_pre = pre_gradient(variant_all, unit_mask, hidden_full)
    grad_gate_up = jnp.einsum(
        "td,tkf->kdf", block_input, grad_pre, preferred_element_type=jnp.float32
    )
    return (grad_gate_up[None], grad_down[None])


def solution(mesh):
    in_specs = (
        P(None, "dp"),
        P(None, "dp", ("group", "mp")),
        P(("group", "mp"), "dp"),
        P("group", None, "dp", "mp"),
        P("group", "mp", "dp"),
        P("group"),
    )
    out_specs = (P("group", None, "dp", "mp"), P("group", "mp", "dp"))
    return jax.shard_map(body, mesh=mesh, in_specs=in_specs, out_specs=out_specs, check_vma=False)
```

profile of v0, /device:TPU:1, one launch (start us, length us, event | category | flops | bytes accessed | tf_op | source)
XLA Modules:
  0.0 652.1 jit_solution(2625803845936884595)
XLA Ops:
  7.2 1.4 copy-done
  8.7 5.2 fusion.45
  13.9 1.1 copy-done.1
  15.0 5.5 fusion.29
  20.5 0.0 all-gather.5.cloned.1.call-start
  20.6 66.0 %reduce-scatter.5.cloned.1.call-done = f32[48,2,896]{2,0,1:T(8,128)} async-done(((f32[768,2,896]{2,0,1:T(8,128)}), f32[48,2,896]{2,0,1:T(8,128)}) %reduce-scatter.5.cloned.1.call-update) | async-done | bytes 344080 | tf_op jit(solution)/shard_map/reduce_scatter | solution.py:40
  86.6 1.0 convert_element_type.66
  87.6 0.7 fusion.52
  88.3 0.0 all-gather.3.cloned.1.call-start
  88.4 71.3 %reduce-scatter.3.cloned.1.call-done = f32[48,2,896]{2,0,1:T(8,128)} async-done(((f32[768,2,896]{2,0,1:T(8,128)}), f32[48,2,896]{2,0,1:T(8,128)}) %reduce-scatter.3.cloned.1.call-update) | async-done | bytes 344080 | tf_op jit(solution)/shard_map/reduce_scatter | solution.py:41
  159.7 1.7 convert_element_type.60
  161.4 38.0 %all-gather.5.cloned.1.call-done = bf16[768,896]{1,0:T(8,128)(2,1)} async-done(((bf16[48,896]{1,0:T(8,128)(2,1)}), bf16[768,896]{1,0:T(8,128)(2,1)}) %all-gather.5.cloned.1.call-update) | async-done | bytes 1376272 | tf_op jit(solution)/shard_map/all_gather | solution.py:47
  199.4 3.7 fusion.57
  203.8 35.3 %all-gather.3.cloned.1.call-done = bf16[768,2,896]{2,0,1:T(8,128)(2,1)} async-done(((bf16[48,2,896]{2,0,1:T(8,128)(2,1)}), bf16[768,2,896]{2,0,1:T(8,128)(2,1)}) %all-gather.3.cloned.1.call-update) | async-done | bytes 2752528 | tf_op jit(solution)/shard_map/all_gather | solution.py:48
  239.1 4.0 fusion.31
  243.2 163.2 %all-reduce.6.cloned.1.call-done = f32[768,512]{1,0:T(8,128)} async-done(((f32[768,512]{1,0:T(8,128)}), f32[768,512]{1,0:T(8,128)}) %all-reduce.6.cloned.1.call-update) | async-done | bytes 1572880 | tf_op jit(solution)/shard_map/psum | solution.py:53
  406.4 93.0 %all-reduce.4.cloned.1.call-done = f32[768,512]{1,0:T(8,128)} async-done(((f32[768,512]{1,0:T(8,128)}), f32[768,512]{1,0:T(8,128)}) %all-reduce.4.cloned.1.call-update) | async-done | bytes 1572880 | tf_op jit(solution)/shard_map/psum | solution.py:54
  499.4 2.3 multiply_convert_fusion
  501.7 3.7 fusion.39
  505.5 4.1 convolution_bitcast_fusion
  509.6 123.6 %all-reduce.8.cloned.1.call-done = f32[768,896]{1,0:T(8,128)} async-done(((f32[768,896]{1,0:T(8,128)}), f32[768,896]{1,0:T(8,128)}) %all-reduce.8.cloned.1.call-update) | async-done | bytes 2752528 | tf_op jit(solution)/shard_map/psum | solution.py:63
  633.2 4.0 fusion.36
  637.2 3.5 fusion.26
  640.7 4.6 copy.9
  (17 shorter events, 0.3 us)
Async XLA Ops:
  7.2 1.5 copy-start
  7.2 79.4 %reduce-scatter.5.cloned.1.call-start = ((), (), s32[]{:S(2)}) async-start(), calls=%async_computation.5 | async-start | bytes 5849088 | tf_op jit(solution)/shard_map/reduce_scatter | solution.py:40
  13.9 1.1 copy-start.1
  13.9 145.8 %reduce-scatter.3.cloned.1.call-start = ((), (), s32[]{:S(2)}) async-start(), calls=%async_computation.2 | async-start | bytes 5849088 | tf_op jit(solution)/shard_map/reduce_scatter | solution.py:41
  20.5 178.9 %all-gather.5.cloned.1.call-start = ((), (), s32[]{:S(2)}) async-start(), calls=%async_computation.6 | async-start | bytes 1462272 | tf_op jit(solution)/shard_map/all_gather | solution.py:47
  88.3 150.8 %all-gather.3.cloned.1.call-start = ((), (), s32[]{:S(2)}) async-start(), calls=%async_computation.3 | async-start | bytes 2924544 | tf_op jit(solution)/shard_map/all_gather | solution.py:48
  161.3 77.8 %copy-start.2 = (bf16[1,896,512]{2,1,0:T(8,128)(2,1)S(1)}, bf16[1,896,512]{2,1,0:T(8,128)(2,1)}, u32[]{:S(2)}) copy-start(bf16[1,896,512]{2,1,0:T(8,128)(2,1)} %param.10) | copy-start | bytes 2752516
  161.4 245.1 %all-reduce.6.cloned.1.call-start = ((), (), s32[]{:S(2)}) async-start(), calls=%async_computation.7 | async-start | bytes 3145728 | tf_op jit(solution)/shard_map/psum | solution.py:53
  203.1 296.3 %all-reduce.4.cloned.1.call-start = ((), (), s32[]{:S(2)}) async-start(), calls=%async_computation.4 | async-start | bytes 3145728 | tf_op jit(solution)/shard_map/psum | solution.py:54
  243.2 390.0 %all-reduce.8.cloned.1.call-start = ((), (), s32[]{:S(2)}) async-start(), calls=%async_computation.8 | async-start | bytes 5505024 | tf_op jit(solution)/shard_map/psum | solution.py:63
Sparse Core Ops, SparseCore 0:
  14.0 72.5 reduce-scatter.4
  89.1 70.4 reduce-scatter.2
  162.1 37.2 all-gather.4
  201.6 37.4 all-gather.2
  242.2 164.1 all-reduce.5
  409.5 89.8 all-reduce.3
  505.6 127.5 all-reduce.7
where the time goes:
time: 653 us; the launch traced here: 652 us
  waiting for transfers between devices  590 us (90%)
  matrix products  29.8 us (5%)
  between operations  14.8 us (2%)
  other arithmetic  9.67 us (1%)
  local copies, waits for them, and re-layouts  7.1 us (1%)
    psum x1, waiting for transfers between devices, body(): teacher = lax.psum(teacher_part, ('group', 'mp'))  163 us
    psum x1, waiting for transfers between devices, body(): hidden_full = lax.psum(hidden_part, 'dp')  124 us
    psum x1, waiting for transfers between devices, body(): student = lax.psum(student_part, 'mp')  93 us
    reduce_scatter x1, waiting for transfers between devices, body(): lax.psum_scatter(variant_term, 'dp', scatter_dimension=0, tiled=True)  71.3 us
    reduce_scatter x1, waiting for transfers between devices, body(): lax.psum_scatter(parent_term, 'dp', scatter_dimension=0, tiled=True)  66 us
    all_gather x1, waiting for transfers between devices, body(): lax.all_gather(parent_hidden, 'dp', axis=0, tiled=True)  38 us
    all_gather x1, waiting for transfers between devices, body(): lax.all_gather(variant_pre, 'dp', axis=0, tiled=True)  35.3 us
  transfers between devices with their start and end apart: 7, of which 7 were waited for; matrix products, arithmetic and copies ran while one was open for 3% of the time, Pallas kernels for 0%

commit v1 on v0

--- a/solution.py
+++ b/solution.py
@@ -50,7 +50,7 @@
     variant_hidden = gated_values(variant_all, unit_mask)
     teacher_part = jnp.dot(parent_all, parent_down, preferred_element_type=jnp.float32)
     student_part = jnp.dot(variant_hidden, local_down, preferred_element_type=jnp.float32)
-    teacher = lax.psum(teacher_part, ("group", "mp"))
+    teacher = lax.psum(lax.psum(teacher_part, "group"), "mp")
     student = lax.psum(student_part, "mp")
     loss_scale = 1.0 / math.sqrt(all_tokens)
     output_grad = ((student - teacher) * loss_scale).astype(jnp.bfloat16)

time: 653 us -> 587 us (0.90)
  waiting for transfers between devices: 590 us -> 525 us
    psum x1, waiting for transfers between devices: 163 us -> 54.1 us  [body(): teacher = lax.psum(lax.psum(teacher_part, 'group'), 'mp')]
    psum x1, waiting for transfers between devices: 93 us -> 130 us  [body(): student = lax.psum(student_part, 'mp')]
    psum x1, waiting for transfers between devices: 124 us -> 130 us  [body(): hidden_full = lax.psum(hidden_part, 'dp')]
  transfers between devices with their start and end apart: 7 -> 7, of which waited for: 7 -> 7; matrix products, arithmetic and copies ran while one was open for 3% -> 4% of each run, Pallas kernels for 0% -> 0%
where the time goes in v1:
time: 587 us
  waiting for transfers between devices  525 us (89%)
  matrix products  29.7 us (5%)
  between operations  14.8 us (3%)
  other arithmetic  9.67 us (2%)
  local copies, waits for them, and re-layouts  7.1 us (1%)
    psum x1, waiting for transfers between devices, body(): student = lax.psum(student_part, 'mp')  130 us
    psum x1, waiting for transfers between devices, body(): hidden_full = lax.psum(hidden_part, 'dp')  130 us
    reduce_scatter x1, waiting for transfers between devices, body(): lax.psum_scatter(variant_term, 'dp', scatter_dimension=0, tiled=True)  71.3 us
    reduce_scatter x1, waiting for transfers between devices, body(): lax.psum_scatter(parent_term, 'dp', scatter_dimension=0, tiled=True)  66 us
    psum x1, waiting for transfers between devices, body(): teacher = lax.psum(lax.psum(teacher_part, 'group'), 'mp')  54.1 us
    all_gather x1, waiting for transfers between devices, body(): lax.all_gather(parent_hidden, 'dp', axis=0, tiled=True)  38 us
    all_gather x1, waiting for transfers between devices, body(): lax.all_gather(variant_pre, 'dp', axis=0, tiled=True)  35.3 us
  transfers between devices with their start and end apart: 7, of which 7 were waited for; matrix products, arithmetic and copies ran while one was open for 4% of the time, Pallas kernels for 0%

profile of v1, /device:TPU:1, one launch (start us, length us, event | category | flops | bytes accessed | tf_op | source)
XLA Modules:
  0.0 586.7 jit_solution(9532788135159649136)
XLA Ops:
  7.2 1.4 copy-done
  8.7 5.2 fusion.45
  13.9 1.1 copy-done.1
  15.0 5.5 fusion.29
  20.5 0.0 all-gather.5.cloned.1.call-start
  20.6 66.0 %reduce-scatter.5.cloned.1.call-done = f32[48,2,896]{2,0,1:T(8,128)} async-done(((f32[768,2,896]{2,0,1:T(8,128)}), f32[48,2,896]{2,0,1:T(8,128)}) %reduce-scatter.5.cloned.1.call-update) | async-done | bytes 344080 | tf_op jit(solution)/shard_map/reduce_scatter | solution.py:40
  86.6 1.0 convert_element_type.66
  87.6 0.7 fusion.52
  88.3 0.0 all-gather.3.cloned.1.call-start
  88.4 71.3 %reduce-scatter.3.cloned.1.call-done = f32[48,2,896]{2,0,1:T(8,128)} async-done(((f32[768,2,896]{2,0,1:T(8,128)}), f32[48,2,896]{2,0,1:T(8,128)}) %reduce-scatter.3.cloned.1.call-update) | async-done | bytes 344080 | tf_op jit(solution)/shard_map/reduce_scatter | solution.py:41
  159.6 1.7 convert_element_type.60
  161.4 38.0 %all-gather.5.cloned.1.call-done = bf16[768,896]{1,0:T(8,128)(2,1)} async-done(((bf16[48,896]{1,0:T(8,128)(2,1)}), bf16[768,896]{1,0:T(8,128)(2,1)}) %all-gather.5.cloned.1.call-update) | async-done | bytes 1376272 | tf_op jit(solution)/shard_map/all_gather | solution.py:47
  199.4 3.7 fusion.57
  203.8 35.3 %all-gather.3.cloned.1.call-done = bf16[768,2,896]{2,0,1:T(8,128)(2,1)} async-done(((bf16[48,2,896]{2,0,1:T(8,128)(2,1)}), bf16[768,2,896]{2,0,1:T(8,128)(2,1)}) %all-gather.3.cloned.1.call-update) | async-done | bytes 2752528 | tf_op jit(solution)/shard_map/all_gather | solution.py:48
  239.1 4.0 fusion.31
  243.1 54.1 %all-reduce.5.cloned.1.call-done = f32[768,512]{1,0:T(8,128)} async-done(((f32[768,512]{1,0:T(8,128)}), f32[768,512]{1,0:T(8,128)}) %all-reduce.5.cloned.1.call-update) | async-done | bytes 1572880 | tf_op jit(solution)/shard_map/psum | solution.py:53
  297.3 130.2 %all-reduce.9.cloned.1.call-done = (f32[768,512]{1,0:T(8,128)}, f32[768,512]{1,0:T(8,128)}) async-done(((f32[768,512]{1,0:T(8,128)}, f32[768,512]{1,0:T(8,128)}), (f32[768,512]{1,0:T(8,128)}, f32[768,512]{1,0:T(8,128)})) %all-reduce.9.cloned.1.call-update) | async-done | bytes 3145744 | tf_op jit(solution)/shard_map/psum | solution.py:54
  427.5 2.3 multiply_convert_fusion
  429.8 3.7 fusion.39
  433.5 4.1 convolution_bitcast_fusion
  437.6 130.2 %all-reduce.7.cloned.1.call-done = f32[768,896]{1,0:T(8,128)} async-done(((f32[768,896]{1,0:T(8,128)}), f32[768,896]{1,0:T(8,128)}) %all-reduce.7.cloned.1.call-update) | async-done | bytes 2752528 | tf_op jit(solution)/shard_map/psum | solution.py:63
  567.8 4.0 fusion.36
  571.8 3.4 fusion.26
  575.3 4.6 copy.9
  (17 shorter events, 0.3 us)
Async XLA Ops:
  7.2 1.5 copy-start
  7.2 79.4 %reduce-scatter.5.cloned.1.call-start = ((), (), s32[]{:S(2)}) async-start(), calls=%async_computation.4 | async-start | bytes 5849088 | tf_op jit(solution)/shard_map/reduce_scatter | solution.py:40
  13.9 1.1 copy-start.1
  13.9 145.8 %reduce-scatter.3.cloned.1.call-start = ((), (), s32[]{:S(2)}) async-start(), calls=%async_computation.2 | async-start | bytes 5849088 | tf_op jit(solution)/shard_map/reduce_scatter | solution.py:41
  20.5 178.9 %all-gather.5.cloned.1.call-start = ((), (), s32[]{:S(2)}) async-start(), calls=%async_computation.5 | async-start | bytes 1462272 | tf_op jit(solution)/shard_map/all_gather | solution.py:47
  88.3 150.8 %all-gather.3.cloned.1.call-start = ((), (), s32[]{:S(2)}) async-start(), calls=%async_computation.3 | async-start | bytes 2924544 | tf_op jit(solution)/shard_map/all_gather | solution.py:48
  161.3 77.8 %copy-start.2 = (bf16[1,896,512]{2,1,0:T(8,128)(2,1)S(1)}, bf16[1,896,512]{2,1,0:T(8,128)(2,1)}, u32[]{:S(2)}) copy-start(bf16[1,896,512]{2,1,0:T(8,128)(2,1)} %param.10) | copy-start | bytes 2752516
  161.3 135.9 %all-reduce.5.cloned.1.call-start = ((), (), s32[]{:S(2)}) async-start(), calls=%async_computation.6 | async-start | bytes 3145728 | tf_op jit(solution)/shard_map/psum | solution.py:53
  203.1 224.4 %all-reduce.9.cloned.1.call-start = ((), (), s32[]{:S(2)}) async-start(), calls=%async_computation.8 | async-start | bytes 6291456 | tf_op jit(solution)/shard_map/psum | solution.py:54
  297.2 270.6 %all-reduce.7.cloned.1.call-start = ((), (), s32[]{:S(2)}) async-start(), calls=%async_computation.7 | async-start | bytes 5505024 | tf_op jit(solution)/shard_map/psum | solution.py:63
Sparse Core Ops, SparseCore 0:
  14.0 72.5 reduce-scatter.4
  89.1 70.4 reduce-scatter.2
  162.1 37.2 all-gather.4
  201.6 37.4 all-gather.2
  241.9 55.2 all-reduce.4
  300.3 127.0 all-reduce.8
  433.6 134.1 all-reduce.6
